TPU v7x, 128 devices: a whole 4x4x4 slice. The times are simulated.
128 devices in a mesh: replica: 1, heads: 64 (over z, y, x), model: 2 (over core).
Axes of the slice: x: 4, y: 4, z: 4, core: 2. Of those that a mesh axis runs over, the one named last changes fastest.
Arguments:
- tokens: bfloat16 [32, 16384], P('replica')
- w_query: bfloat16 [16384, 16384], P(None, ('heads', 'model'))
- w_key: bfloat16 [16384, 1024], replicated
- w_value: bfloat16 [16384, 1024], replicated
- w_out: bfloat16 [16384, 16384], P(('heads', 'model'))
- key_cache: bfloat16 [32, 8, 2048, 128], P(('replica', 'model'))
- value_cache: bfloat16 [32, 8, 2048, 128], P(('replica', 'model'))
- lengths: int32 [32], P(('replica', 'model'))
Outputs:
- output 1: bfloat16 [32, 16384], P('replica')
- output 2: bfloat16 [32, 8, 128], P(('replica', 'model'))
- output 3: bfloat16 [32, 8, 128], P(('replica', 'model'))
All inputs are finite; a program needn't handle non-finite values.
Results may differ from a plain program's by a relative error of at most 0.00215798.
Values are sent between devices in bfloat16 or wider.
A program may use at most 1 GiB of HBM per device.

v0:
```python
import jax
import jax.numpy as jnp
from jax import lax
from jax.sharding import PartitionSpec as P


def attend(queries, key_rows, value_rows, key_last, value_last, seq_len):
    score_scale = queries.shape[-1] ** -0.5
    scores = jnp.einsum("bgrd,bgtd->bgrt", queries, key_rows, preferred_element_type=jnp.float32) * score_scale
    score_new = jnp.einsum("bgrd,bgd->bgr", queries, key_last, preferred_element_type=jnp.float32) * score_scale
    positions = lax.broadcasted_iota(jnp.int32, (1, 1, 1, key_rows.shape[2]), 3)
    scores = jnp.where(positions < seq_len[:, None, None, None], scores, -jnp.inf)
    score_max = jnp.maximum(jnp.max(scores, axis=-1), score_new)
    weights = jnp.exp(scores - score_max[..., None])
    weight_new = jnp.exp(score_new - score_max)
    denom_sum = jnp.sum(weights, axis=-1) + weight_new
    weighted_sum = jnp.einsum("bgrt,bgtd->bgrd", weights.astype(jnp.bfloat16), value_rows, preferred_element_type=jnp.float32)
    weighted_sum = weighted_sum + weight_new.astype(jnp.bfloat16).astype(jnp.float32)[..., None] * value_last.astype(jnp.float32)[:, :, None, :]
    return (weighted_sum / denom_sum[..., None]).astype(jnp.bfloat16)


def solution(mesh):
    heads_count = mesh.shape["heads"]
    model_count = mesh.shape["model"]

    def local_step(tokens, w_query, w_key, w_value, w_out, key_cache, value_cache, lengths):
        batch_all = tokens.shape[0]
        local_rows = key_cache.shape[0]
        kv_count = key_cache.shape[1]
        head_dim = key_cache.shape[3]
        heads_local = w_query.shape[1] // head_dim
        heads_shard = heads_local * model_count
        group_size = heads_shard * heads_count // kv_count
        shard_groups = max(1, heads_shard // group_size)
        head_index = lax.axis_index("heads")
        model_index = lax.axis_index("model")
        queries = jnp.dot(tokens, w_query, preferred_element_type=jnp.float32).astype(jnp.bfloat16)
        queries = lax.all_to_all(queries.reshape(batch_all, heads_local, head_dim), "model", 0, 1, tiled=True)
        own_tokens = lax.dynamic_slice_in_dim(tokens, model_index * local_rows, local_rows, 0)
        key_new = jnp.dot(own_tokens, w_key, preferred_element_type=jnp.float32).astype(jnp.bfloat16)
        key_new = key_new.reshape(local_rows, kv_count, head_dim)
        value_new = jnp.dot(own_tokens, w_value, preferred_element_type=jnp.float32).astype(jnp.bfloat16)
        value_new = value_new.reshape(local_rows, kv_count, head_dim)
        first_group = head_index * heads_shard // group_size
        attended = attend(
            queries.reshape(local_rows, shard_groups, heads_shard // shard_groups, head_dim),
            lax.dynamic_slice_in_dim(key_cache, first_group, shard_groups, 1),
            lax.dynamic_slice_in_dim(value_cache, first_group, shard_groups, 1),
            lax.dynamic_slice_in_dim(key_new, first_group, shard_groups, 1),
            lax.dynamic_slice_in_dim(value_new, first_group, shard_groups, 1),
            lengths,
        )
        attended = lax.all_to_all(attended.reshape(local_rows, heads_shard, head_dim), "model", 1, 0, tiled=True)
        partial = jnp.dot(attended.reshape(batch_all, heads_local * head_dim), w_out, preferred_element_type=jnp.float32)
        mixed_sum = lax.psum(partial, ("heads", "model"))
        out_tokens = (tokens.astype(jnp.float32) + mixed_sum).astype(jnp.bfloat16)
        return (out_tokens, key_new, value_new)

    cache_spec = P(("replica", "model"), None, None, None)
    new_spec = P(("replica", "model"), None, None)
    return jax.shard_map(
        local_step,
        mesh=mesh,
        in_specs=(P("replica", None), P(None, ("heads", "model")), P(None, None), P(None, None), P(("heads", "model"), None), cache_spec, cache_spec, P(("replica", "model"))),
        out_specs=(P("replica", None), new_spec, new_spec),
        check_vma=False,
    )
```

profile of v0, /device:TPU:1, one launch (start us, length us, event | category | flops | bytes accessed | tf_op | source)
XLA Modules:
  0.0 226.6 jit_solution(15154690009212352573)
XLA Ops:
  7.2 3.3 %fusion.17 = bf16[32,1,128]{2,0,1:T(8,128)(2,1)S(1)} fusion(bf16[32,16384]{1,0:T(8,128)(2,1)} %param.8, bf16[16384,128]{1,0:T(8,128)(2,1)} %param.9), kind=kOutput, calls=%fused_computation.15 | convolution fusion | flops 134221824 | bytes 5251072 | tf_op jit(solution)/shard_map/dot_general | solution.py:37
  10.4 0.5 broadcast.30
  11.0 0.6 reduce.4
  11.6 0.6 reshape.115
  12.2 4.6 %all-to-all-start = ((bf16[2,2,1024]{2,1,0:T(2,128)(2,1)}), bf16[2,2,1024]{2,1,0:T(2,128)(2,1)S(1)}, u32[]{:S(2)}, u32[]{:S(2)}) async-start(bf16[2,2,1024]{2,1,0:T(2,128)(2,1)} %reshape.115), calls=%async_computation | async-start | bytes 16384 | tf_op jit(solution)/shard_map/all_to_all | solution.py:38
  16.8 0.0 all-reduce.2.cloned.1.call-start
  16.8 0.8 all-to-all-done
  17.6 0.0 copy-start
  17.7 15.2 %fusion.12 = bf16[2,8,8,128]{3,1,2,0:T(8,128)(2,1)S(1)} fusion(bf16[16384,1024]{1,0:T(8,128)(2,1)} %param.10, bf16[32,16384]{1,0:T(8,128)(2,1)} %param.8, s32[]{:T(128)S(6)} %select_n.22), kind=kOutput, calls=%fused_computation.11 | convolution fusion | flops 536887296 | bytes 34111492 | tf_op jit(solution)/shard_map/dot_general | solution.py:40
  32.9 0.0 copy-start.2
  33.0 0.0 copy-done
  33.0 0.0 copy-start.4
  33.0 12.8 %fusion.13 = bf16[2,8,8,128]{3,1,2,0:T(8,128)(2,1)S(1)} fusion(bf16[16384,1024]{1,0:T(8,128)(2,1)} %param.11, bf16[32,16384]{1,0:T(8,128)(2,1)S(1)} %copy-done, s32[]{:T(128)S(6)} %select_n.22), kind=kOutput, calls=%fused_computation.12 | convolution fusion | flops 536887296 | bytes 34111492 | tf_op jit(solution)/shard_map/dot_general | solution.py:42
  45.8 0.0 copy-start.3
  45.9 0.1 iota_compare_fusion
  46.0 0.1 fusion.30
  46.1 5.9 %fusion.37 = (f32[16,2]{1,0:T(8,128)S(1)}, f32[16,2,2048]{2,1,0:T(2,128)S(1)}) fusion(bf16[16,8,2048,128]{3,2,1,0:T(8,128)(2,1)} %param.13, s32[]{:T(128)S(6)} %select_n.20, bf16[2,16,1,128]{3,1,0,2:T(8,128)(2,1)S(1)} %bitcast.62, pred[16,2048]{1,0:T(8,128)(4,1)S(1)} %iota_compare_fusion), kind=kOutput, calls=%fused_computation.39 | convolution fusion | flops 16973792 | bytes 8691844 | tf_op jit(solution)/shard_map/bgrd,bgtd->bgrt/dot_general | solution.py:9
  52.0 0.3 fusion.26
  52.4 4.7 %fusion.21 = bf16[16,2,128]{2,1,0:T(2,128)(2,1)S(1)} fusion(bf16[16,8,2048,128]{3,2,1,0:T(8,128)(2,1)} %param.14, s32[]{:T(128)S(6)} %select_n.20, f32[16,2,2048]{2,1,0:T(2,128)S(1)} %get-tuple-element.6, f32[16,2]{1,0:T(8,128)S(1)} %multiply_maximum_fusion, f32[16,2]{1,0:T(8,128)S(1)} %get-tuple-element.4, f32[16,128]{1,0:T(8,128)S(1)} %bitcast.57, ...), kind=kOutput, calls=%fused_computation.17 | convolution fusion | flops 16924672 | bytes 8667524 | tf_op jit(solution)/shard_map/bgrt,bgtd->bgrd/dot_general | solution.py:17
  57.0 3.7 %all_to_all.30 = bf16[16,2,128]{2,0,1:T(8,128)(2,1)S(1)} all-to-all(bf16[16,2,128]{2,0,1:T(8,128)(2,1)S(1)} %copy.21), channel_id=1, replica_groups=mesh['replica'=1,'heads'=64,'model'=2] {'model'}, dimensions={1} | all-to-all | bytes 16384 | tf_op jit(solution)/shard_map/all_to_all | solution.py:53
  60.8 2.0 fusion.38
  62.8 0.0 all-reduce.2.cloned.1.call-update
  62.8 154.3 %all-reduce.2.cloned.1.call-done = f32[32,16384]{1,0:T(8,128)} async-done(((f32[32,16384]{1,0:T(8,128)}), f32[32,16384]{1,0:T(8,128)}) %all-reduce.2.cloned.1.call-update) | async-done | bytes 2097168 | tf_op jit(solution)/shard_map/psum | solution.py:55
  217.1 2.7 %add_convert_fusion = bf16[32,16384]{1,0:T(8,128)(2,1)} fusion(f32[32,16384]{1,0:T(8,128)} %all-reduce.2.cloned.1.call-done, bf16[32,16384]{1,0:T(8,128)(2,1)S(1)} %copy-done), kind=kLoop, calls=%fused_computation.8 | loop fusion | flops 1572864 | bytes 4194304 | tf_op jit(solution)/shard_map/convert_element_type | solution.py:56
  (15 shorter events, 0.1 us)
Async XLA Ops:
  12.2 5.4 %all-to-all-start = ((bf16[2,2,1024]{2,1,0:T(2,128)(2,1)}), bf16[2,2,1024]{2,1,0:T(2,128)(2,1)S(1)}, u32[]{:S(2)}, u32[]{:S(2)}) async-start(bf16[2,2,1024]{2,1,0:T(2,128)(2,1)} %reshape.115), calls=%async_computation | async-start | bytes 16384 | tf_op jit(solution)/shard_map/all_to_all | solution.py:38
  16.8 200.3 %all-reduce.2.cloned.1.call-start = ((), (), s32[]{:S(2)}) async-start(), calls=%async_computation.2 | async-start | bytes 4194304 | tf_op jit(solution)/shard_map/psum | solution.py:55
  17.6 15.3 %copy-start = (bf16[32,16384]{1,0:T(8,128)(2,1)S(1)}, bf16[32,16384]{1,0:T(8,128)(2,1)}, u32[]{:S(2)}) copy-start(bf16[32,16384]{1,0:T(8,128)(2,1)} %param.8) | copy-start | bytes 3145732
  32.9 12.9 %copy-start.2 = (bf16[2,8,8,128]{3,2,1,0:T(8,128)(2,1)}, bf16[2,8,8,128]{3,2,1,0:T(8,128)(2,1)S(1)}, u32[]{:S(2)}) copy-start(bf16[2,8,8,128]{3,2,1,0:T(8,128)(2,1)S(1)} %copy.26) | copy-start | bytes 98308
  33.0 12.9 %copy-start.4 = (s32[16]{0:T(128)S(1)}, s32[16]{0:T(128)}, u32[]{:S(2)}) copy-start(s32[16]{0:T(128)} %param.15) | copy-start | bytes 196
  45.8 11.2 %copy-start.3 = (bf16[2,8,8,128]{3,2,1,0:T(8,128)(2,1)}, bf16[2,8,8,128]{3,2,1,0:T(8,128)(2,1)S(1)}, u32[]{:S(2)}) copy-start(bf16[2,8,8,128]{3,2,1,0:T(8,128)(2,1)S(1)} %copy.27) | copy-start | bytes 98308
  46.1 14.7 %copy-start.1 = (bf16[128,16384]{1,0:T(8,128)(2,1)S(1)}, bf16[128,16384]{1,0:T(8,128)(2,1)}, u32[]{:S(2)}) copy-start(bf16[128,16384]{1,0:T(8,128)(2,1)} %param.12) | copy-start | bytes 12582916
Sparse Core Ops, SparseCore 0:
  62.9 154.1 all-reduce.1
where the time goes:
time: 227 us
  waiting for transfers between devices  155 us (68%)
  matrix products  44 us (19%)
  between operations  14.2 us (6%)
  starting transfers between devices  4.57 us (2%)
  other arithmetic  3.84 us (2%)
  blocking collectives  3.71 us (2%)
    psum x1, waiting for transfers between devices, local_step(): mixed_sum = lax.psum(partial, ('heads', 'model'))  154 us
    dot_general x1, matrix products, local_step(): jnp.dot(own_tokens, w_key, preferred_element_type=jnp.float32)  15.2 us
    dot_general x1, matrix products, local_step(): jnp.dot(own_tokens, w_value, preferred_element_type=jnp.float32)  12.8 us
    dot_general x1, matrix products, attend(): jnp.einsum('bgrd,bgtd->bgrt', queries, key_rows, preferred_element_type=j...  5.9 us
    dot_general x1, matrix products, attend(): jnp.einsum('bgrt,bgtd->bgrd', weights.astype(jnp.bfloat16), value_rows, p...  4.68 us
    all_to_all x1, starting transfers between devices, local_step(): lax.all_to_all(queries.reshape(batch_all, heads_local, head_dim), 'model'...  4.57 us
  transfers between devices with their start and end apart: 2, of which 2 were waited for; matrix products, arithmetic and copies ran while one was open for 0% of the time, Pallas kernels for 0%

commit v1 on v0

--- a/solution.py
+++ b/solution.py
@@ -1,7 +1,14 @@
+import functools
+
 import jax
 import jax.numpy as jnp
 from jax import lax
+from jax.experimental import pallas as pl
+from jax.experimental.pallas import tpu as pltpu
 from jax.sharding import PartitionSpec as P
+
+MESH = pl.DeviceIdType.MESH
+ROTATIONS = ((0, 1, 2), (1, 2, 0), (2, 0, 1))
 
 
 def attend(queries, key_rows, value_rows, key_last, value_last, seq_len):
@@ -17,6 +24,195 @@
     weighted_sum = jnp.einsum("bgrt,bgtd->bgrd", weights.astype(jnp.bfloat16), value_rows, preferred_element_type=jnp.float32)
     weighted_sum = weighted_sum + weight_new.astype(jnp.bfloat16).astype(jnp.float32)[..., None] * value_last.astype(jnp.float32)[:, :, None, :]
     return (weighted_sum / denom_sum[..., None]).astype(jnp.bfloat16)
+
+
+def pick(rot, values):
+    if isinstance(rot, int):
+        return values[rot]
+    return jnp.where(rot == 0, values[0], jnp.where(rot == 1, values[1], values[2]))
+
+
+def peer_along(rot, place, coord, step):
+    out = []
+    for dims in ROTATIONS:
+        dim = dims[place]
+        moved = [coord[0], coord[1], coord[2]]
+        moved[dim] = lax.rem(coord[dim] + step, 4)
+        out.append((moved[2] * 4 + moved[1]) * 4 + moved[0])
+    return pick(rot, out)
+
+
+def coord_along(rot, place, coord):
+    return pick(rot, [coord[dims[place]] for dims in ROTATIONS])
+
+
+def mix_kernel(o_ref, w_ref, tok_ref, out_ref, wbuf, part, r1, acc1, r2, acc2, r3, fin, tokbuf, agbuf,
+               wsem, wsend, wrecv, s1, v1, s2, v2, s3, v3, ag_s, ag_v, dd_s, dd_v):
+    core = lax.axis_index("model")
+    chip = lax.axis_index("heads")
+    coord = (lax.rem(chip, 4), lax.rem(lax.div(chip, 4), 4), lax.div(chip, 16))
+    half = 8192
+    my_col = pl.multiple_of(core * half, half)
+    other_col = pl.multiple_of((1 - core) * half, half)
+    my_row = pl.multiple_of(core * 128, 128)
+
+    w_local = pltpu.make_async_copy(w_ref.at[:, pl.ds(my_col, half)], wbuf.at[pl.ds(my_row, 128)], wsem.at[0])
+    w_local.start()
+    t_local = pltpu.make_async_copy(
+        tok_ref.at[:, pl.ds(pl.multiple_of(core * half + chip * 128, 128), 128)], tokbuf, wsem.at[1])
+    t_local.start()
+
+    barrier = pltpu.get_barrier_semaphore()
+    pl.semaphore_signal(barrier, inc=1, device_id={"heads": chip, "model": 1 - core}, device_id_type=MESH)
+    for place in range(3):
+        for k in (1, 2, 3):
+            pl.semaphore_signal(
+                barrier, inc=1, device_id={"heads": peer_along(0, place, coord, k), "model": core}, device_id_type=MESH)
+    pl.semaphore_wait(barrier, 10)
+
+    w_remote = pltpu.make_async_remote_copy(
+        src_ref=w_ref.at[:, pl.ds(other_col, half)], dst_ref=wbuf.at[pl.ds(my_row, 128)],
+        send_sem=wsend, recv_sem=wrecv, device_id={"heads": chip, "model": 1 - core}, device_id_type=MESH)
+    w_remote.start()
+
+    rots = (0, 1, 2, core)
+    w_local.wait()
+    w_remote.wait_recv()
+    o = o_ref[...]
+
+    @pl.loop(0, 16)
+    def _(t):
+        bz, by = lax.div(t, 4), lax.rem(t, 4)
+        res = jnp.dot(o, wbuf[:, pl.ds(pl.multiple_of(t * 512, 512), 512)], preferred_element_type=jnp.float32)
+        for bx in range(4):
+            block = (bx, by, bz)
+            for rg in range(4):
+                at = pick(rots[rg], [block[d[0]] * 16 + block[d[1]] * 4 + block[d[2]] for d in ROTATIONS])
+                part[rg, at] = res[rg * 8:rg * 8 + 8, bx * 128:bx * 128 + 128]
+
+    def exchange(rg, place, src, width, dst, ssem, rsem):
+        copies = []
+        mine = coord_along(rots[rg], place, coord)
+        for k in (1, 2, 3):
+            there = lax.rem(mine + k, 4)
+            copy = pltpu.make_async_remote_copy(
+                src_ref=src.at[rg, pl.ds(there * width, width)], dst_ref=dst.at[rg, k - 1],
+                send_sem=ssem.at[rg, k - 1], recv_sem=rsem.at[rg, k - 1],
+                device_id={"heads": peer_along(rots[rg], place, coord, k), "model": core}, device_id_type=MESH)
+            copy.start()
+            copies.append(copy)
+        return copies
+
+    def collect(rg, place, src, width, dst, copies):
+        for copy in copies:
+            copy.wait_recv()
+        mine = coord_along(rots[rg], place, coord)
+        return src[rg, pl.ds(mine * width, width)] + dst[rg, 0] + dst[rg, 1] + dst[rg, 2]
+
+    sent = []
+    c1 = [exchange(rg, 0, part, 16, r1, s1, v1) for rg in range(4)]
+    c2 = []
+    for rg in range(4):
+        acc1[rg] = collect(rg, 0, part, 16, r1, c1[rg])
+        c2.append(exchange(rg, 1, acc1, 4, r2, s2, v2))
+    c3 = []
+    for rg in range(4):
+        acc2[rg] = collect(rg, 1, acc1, 4, r2, c2[rg])
+        c3.append(exchange(rg, 2, acc2, 1, r3, s3, v3))
+    for rg in range(4):
+        fin[pl.ds(rg * 8, 8)] = collect(rg, 2, acc2, 1, r3, c3[rg])[0]
+    for group in (c1, c2, c3):
+        for copies in group:
+            sent += copies
+    t_local.wait()
+    block = (tokbuf[...].astype(jnp.float32) + fin[...]).astype(jnp.bfloat16)
+
+    def ag_rot(cc, h):
+        return (cc * 2 + h) % 3 if isinstance(cc, int) else (h if h == 0 else None)
+
+    halves = []
+    for h in range(2):
+        rot = jnp.where(core == 0, ag_rot(0, h), ag_rot(1, h))
+        a, b, c = (coord_along(rot, i, coord) for i in range(3))
+        halves.append((rot, a, b, c))
+        agbuf[core, h, c * 16 + b * 4 + a] = block[h * 16:h * 16 + 16]
+
+    def spread(h, place, start, width):
+        rot = halves[h][0]
+        copies = []
+        for k in (1, 2, 3):
+            ref = agbuf.at[core, h, pl.ds(start, width)]
+            copy = pltpu.make_async_remote_copy(
+                src_ref=ref, dst_ref=ref, send_sem=ag_s.at[h, place, k - 1], recv_sem=ag_v.at[h, place, k - 1],
+                device_id={"heads": peer_along(rot, place, coord, k), "model": core}, device_id_type=MESH)
+            copy.start()
+            copies.append(copy)
+        return copies
+
+    def across(h, k, start):
+        ref = agbuf.at[core, h, pl.ds(start, 16)]
+        copy = pltpu.make_async_remote_copy(
+            src_ref=ref, dst_ref=ref, send_sem=dd_s.at[h, k], recv_sem=dd_v.at[h, k],
+            device_id={"heads": chip, "model": 1 - core}, device_id_type=MESH)
+        copy.start()
+        return copy
+
+    def arrive(h, place, k, width, base, stride, copy):
+        copy.wait_recv()
+
+    ga = [spread(h, 0, halves[h][3] * 16 + halves[h][2] * 4 + halves[h][1], 1) for h in range(2)]
+    gb = []
+    for h in range(2):
+        for copy in ga[h]:
+            copy.wait_recv()
+        gb.append(spread(h, 1, halves[h][3] * 16 + halves[h][2] * 4, 4))
+    gc, gd = [], []
+    for h in range(2):
+        for copy in gb[h]:
+            copy.wait_recv()
+        gc.append(spread(h, 2, halves[h][3] * 16, 16))
+        gd.append([across(h, 0, halves[h][3] * 16)])
+    for k in (1, 3, 2):
+        for h in range(2):
+            gc[h][k - 1].wait_recv()
+            gd[h].append(across(h, k, lax.rem(halves[h][3] + 4 - k, 4) * 16))
+    for h in range(2):
+        for copy in gd[h]:
+            copy.wait_recv()
+    for cc in range(2):
+        for h in range(2):
+            dims = ROTATIONS[ag_rot(cc, h)]
+            for bz in range(4):
+                for by in range(4):
+                    for bx in range(4):
+                        b = (bx, by, bz)
+                        at = b[dims[2]] * 16 + b[dims[1]] * 4 + b[dims[0]]
+                        col = cc * half + ((bz * 4 + by) * 4 + bx) * 128
+                        out_ref[h * 16:h * 16 + 16, col:col + 128] = agbuf[cc, h, at]
+    w_remote.wait_send()
+    for copies in (*ga, *gb, *gc, *gd, sent):
+        for copy in copies:
+            copy.wait_send()
+
+
+def mix(o, w_out, tokens):
+    f32, bf16 = jnp.float32, jnp.bfloat16
+    dma = pltpu.SemaphoreType.DMA
+    return pl.pallas_call(
+        mix_kernel,
+        out_shape=jax.ShapeDtypeStruct((32, 16384), bf16),
+        in_specs=[pl.BlockSpec(memory_space=pltpu.VMEM), pl.BlockSpec(memory_space=pl.ANY), pl.BlockSpec(memory_space=pl.ANY)],
+        out_specs=pl.BlockSpec(memory_space=pltpu.VMEM),
+        scratch_shapes=[
+            pltpu.VMEM((256, 8192), bf16), pltpu.VMEM((4, 64, 8, 128), f32), pltpu.VMEM((4, 3, 16, 8, 128), f32),
+            pltpu.VMEM((4, 16, 8, 128), f32), pltpu.VMEM((4, 3, 4, 8, 128), f32), pltpu.VMEM((4, 4, 8, 128), f32),
+            pltpu.VMEM((4, 3, 1, 8, 128), f32), pltpu.VMEM((32, 128), f32), pltpu.VMEM((32, 128), bf16),
+            pltpu.VMEM((2, 2, 64, 16, 128), bf16),
+            dma((2,)), dma, dma, dma((4, 3)), dma((4, 3)), dma((4, 3)), dma((4, 3)), dma((4, 3)), dma((4, 3)),
+            dma((2, 3, 3)), dma((2, 3, 3)), dma((2, 4)), dma((2, 4)),
+        ],
+        compiler_params=pltpu.CompilerParams(collective_id=0, has_side_effects=True),
+    )(o, w_out, tokens)
 
 
 def solution(mesh):
@@ -50,10 +246,8 @@
             lax.dynamic_slice_in_dim(value_new, first_group, shard_groups, 1),
             lengths,
         )
-        attended = lax.all_to_all(attended.reshape(local_rows, heads_shard, head_dim), "model", 1, 0, tiled=True)
-        partial = jnp.dot(attended.reshape(batch_all, heads_local * head_dim), w_out, preferred_element_type=jnp.float32)
-        mixed_sum = lax.psum(partial, ("heads", "model"))
-        out_tokens = (tokens.astype(jnp.float32) + mixed_sum).astype(jnp.bfloat16)
+        attended = lax.all_gather(attended.reshape(local_rows, heads_shard * head_dim), "model", axis=0, tiled=True)
+        out_tokens = mix(attended, w_out, tokens)
         return (out_tokens, key_new, value_new)
 
     cache_spec = P(("replica", "model"), None, None, None)

time: 227 us -> 98.8 us (0.44)
  waiting for transfers between devices: 155 us -> 0.82 us
  Pallas kernels: 0 us -> 44 us
  between operations: 14.2 us -> 0.77 us
  other arithmetic: 3.84 us -> 1.1 us
    psum x1 -> x0, waiting for transfers between devices: 154 us -> none  [local_step(): mixed_sum = lax.psum(partial, ('heads', 'model'))]
    pallas_call x0 -> x1, Pallas kernels: none -> 44 us  [mix(): pl.pallas_call(mix_kernel, out_shape=jax.ShapeDtypeStruct((32, 16384), bf...]
    all_to_all x1 -> x0, blocking collectives: 3.71 us -> none  [local_step(): lax.all_to_all(attended.reshape(local_rows, heads_shard, head_dim), 'mode...]
    convert_element_type x1 -> x0, other arithmetic: 2.73 us -> none  [local_step(): out_tokens = (tokens.astype(jnp.float32) + mixed_sum).astype(jnp.bfloat16)]
  transfers between devices with their start and end apart: 2 -> 1, of which waited for: 2 -> 1; matrix products, arithmetic and copies ran while one was open for 0% -> 0% of each run, Pallas kernels for 0% -> 0%
where the time goes in v1:
time: 98.8 us; the launch traced here: 98.5 us
  Pallas kernels  44 us (45%)
  matrix products  41.9 us (42%)
  starting transfers between devices  4.58 us (5%)
  local copies, waits for them, and re-layouts  3.48 us (4%)
  blocking collectives  1.82 us (2%)
  other arithmetic  1.1 us (1%)
    pallas_call x1, Pallas kernels, mix(): pl.pallas_call(mix_kernel, out_shape=jax.ShapeDtypeStruct((32, 16384), bf...  44 us
    dot_general x1, matrix products, local_step(): jnp.dot(own_tokens, w_key, preferred_element_type=jnp.float32)  15.2 us
    dot_general x1, matrix products, local_step(): jnp.dot(own_tokens, w_value, preferred_element_type=jnp.float32)  12.8 us
    dot_general x1, matrix products, attend(): jnp.einsum('bgrd,bgtd->bgrt', queries, key_rows, preferred_element_type=j...  5.75 us
    dot_general x1, matrix products, attend(): jnp.einsum('bgrt,bgtd->bgrd', weights.astype(jnp.bfloat16), value_rows, p...  4.65 us
    all_to_all x1, starting transfers between devices, local_step(): lax.all_to_all(queries.reshape(batch_all, heads_local, head_dim), 'model'...  4.58 us
    dot_general x1, matrix products, local_step(): jnp.dot(tokens, w_query, preferred_element_type=jnp.float32)  3.34 us
    unnamed x16, local copies, waits for them, and re-layouts  2.95 us
  transfers between devices with their start and end apart: 1, of which 1 were waited for; matrix products, arithmetic and copies ran while one was open for 0% of the time, Pallas kernels for 0%

profile of v1, /device:TPU:1, one launch (start us, length us, event | category | flops | bytes accessed | tf_op | source)
XLA Modules:
  0.0 98.5 jit_solution(5915219990504823395)
XLA Ops:
  0.6 0.0 copy-start
  0.6 3.3 %fusion.17 = bf16[32,1,128]{2,0,1:T(8,128)(2,1)S(1)} fusion(bf16[32,16384]{1,0:T(8,128)(2,1)} %tok_ref.1, bf16[16384,128]{1,0:T(8,128)(2,1)} %param.9), kind=kOutput, calls=%fused_computation.14 | convolution fusion | flops 134221824 | bytes 5251072 | tf_op jit(solution)/shard_map/dot_general | solution.py:233
  4.0 0.5 broadcast.30
  4.5 0.6 reduce.4
  5.2 0.6 reshape.113
  5.8 4.6 %all-to-all-start = ((bf16[2,2,1024]{2,1,0:T(2,128)(2,1)}), bf16[2,2,1024]{2,1,0:T(2,128)(2,1)S(1)}, u32[]{:S(2)}, u32[]{:S(2)}) async-start(bf16[2,2,1024]{2,1,0:T(2,128)(2,1)} %reshape.113), calls=%async_computation | async-start | bytes 16384 | tf_op jit(solution)/shard_map/all_to_all | solution.py:234
  10.3 0.8 all-to-all-done
  11.2 0.0 copy-start.3
  11.2 15.2 %fusion.12 = bf16[2,8,8,128]{3,1,2,0:T(8,128)(2,1)S(1)} fusion(bf16[16384,1024]{1,0:T(8,128)(2,1)} %param.10, bf16[32,16384]{1,0:T(8,128)(2,1)} %tok_ref.1, s32[]{:T(128)S(6)} %select_n.22), kind=kOutput, calls=%fused_computation.10 | convolution fusion | flops 536887296 | bytes 34111492 | tf_op jit(solution)/shard_map/dot_general | solution.py:236
  26.4 0.0 copy-start.1
  26.4 0.0 copy-done
  26.5 12.8 %fusion.13 = bf16[2,8,8,128]{3,1,2,0:T(8,128)(2,1)S(1)} fusion(bf16[16384,1024]{1,0:T(8,128)(2,1)} %param.11, bf16[32,16384]{1,0:T(8,128)(2,1)S(1)} %copy-done, s32[]{:T(128)S(6)} %select_n.22), kind=kOutput, calls=%fused_computation.11 | convolution fusion | flops 536887296 | bytes 34111492 | tf_op jit(solution)/shard_map/dot_general | solution.py:238
  39.3 0.0 copy-start.2
  39.3 0.0 copy-done.3
  39.3 0.1 iota_compare_fusion
  39.4 0.1 fusion.30
  39.6 5.7 %fusion.37 = (f32[16,2]{1,0:T(8,128)S(1)}, f32[16,2,2048]{2,1,0:T(2,128)S(1)}) fusion(bf16[16,8,2048,128]{3,2,1,0:T(8,128)(2,1)} %param.13, s32[]{:T(128)S(6)} %select_n.20, bf16[2,16,1,128]{3,1,0,2:T(8,128)(2,1)S(1)} %bitcast.60, pred[16,2048]{1,0:T(8,128)(4,1)S(1)} %iota_compare_fusion), kind=kOutput, calls=%fused_computation.39 | convolution fusion | flops 16973792 | bytes 8691844 | tf_op jit(solution)/shard_map/bgrd,bgtd->bgrt/dot_general | solution.py:16
  45.3 0.3 fusion.26
  45.7 4.7 %fusion.21 = bf16[16,2,128]{2,1,0:T(2,128)(2,1)S(1)} fusion(bf16[16,8,2048,128]{3,2,1,0:T(8,128)(2,1)} %param.14, s32[]{:T(128)S(6)} %select_n.20, f32[16,2,2048]{2,1,0:T(2,128)S(1)} %get-tuple-element.6, f32[16,2]{1,0:T(8,128)S(1)} %multiply_maximum_fusion, f32[16,2]{1,0:T(8,128)S(1)} %get-tuple-element.4, f32[16,128]{1,0:T(8,128)S(1)} %bitcast.54, ...), kind=kOutput, calls=%fused_computation.16 | convolution fusion | flops 16924672 | bytes 8667524 | tf_op jit(solution)/shard_map/bgrt,bgtd->bgrd/dot_general | solution.py:24
  50.3 1.8 %all_gather.3.o_ref = bf16[32,256]{1,0:T(8,128)(2,1)} all-gather(bf16[16,256]{1,0:T(8,128)(2,1)S(1)} %bitcast.58), channel_id=1, replica_groups=mesh['replica'=1,'heads'=64,'model'=2] {'model'}, dimensions={0}, use_global_device_ids=true | all-gather | bytes 24576 | tf_op jit(solution)/shard_map/all_gather | solution.py:249
  52.1 44.0 %shard_map.103 = bf16[32,16384]{1,0:T(8,128)(2,1)} custom-call(bf16[32,256]{1,0:T(8,128)(2,1)} %all_gather.3.o_ref, bf16[128,16384]{1,0:T(8,128)(2,1)} %w_ref.1, bf16[32,16384]{1,0:T(8,128)(2,1)} %tok_ref.1), custom_call_target="tpu_custom_call" | custom-call | tf_op jit(solution)/shard_map/pallas_call | solution.py:201
  96.2 2.3 %copy.39 = bf16[32,16384]{1,0:T(8,128)(2,1)} copy(bf16[32,16384]{1,0:T(8,128)(2,1)} %shard_map.103) | data formatting | bytes 2097152
  98.4 0.0 copy-done.1
  98.4 0.0 copy-done.2
  (10 shorter events, 0.1 us)
Async XLA Ops:
  0.6 25.8 %copy-start = (bf16[32,16384]{1,0:T(8,128)(2,1)S(1)}, bf16[32,16384]{1,0:T(8,128)(2,1)}, u32[]{:S(2)}) copy-start(bf16[32,16384]{1,0:T(8,128)(2,1)} %tok_ref.1) | copy-start | bytes 3145732
  5.8 5.4 %all-to-all-start = ((bf16[2,2,1024]{2,1,0:T(2,128)(2,1)}), bf16[2,2,1024]{2,1,0:T(2,128)(2,1)S(1)}, u32[]{:S(2)}, u32[]{:S(2)}) async-start(bf16[2,2,1024]{2,1,0:T(2,128)(2,1)} %reshape.113), calls=%async_computation | async-start | bytes 16384 | tf_op jit(solution)/shard_map/all_to_all | solution.py:234
  11.2 28.1 %copy-start.3 = (s32[16]{0:T(128)S(1)}, s32[16]{0:T(128)}, u32[]{:S(2)}) copy-start(s32[16]{0:T(128)} %param.15) | copy-start | bytes 196
  26.4 72.1 %copy-start.1 = (bf16[2,8,8,128]{3,2,1,0:T(8,128)(2,1)}, bf16[2,8,8,128]{3,2,1,0:T(8,128)(2,1)S(1)}, u32[]{:S(2)}) copy-start(bf16[2,8,8,128]{3,2,1,0:T(8,128)(2,1)S(1)} %copy.23) | copy-start | bytes 98308
  39.3 59.1 %copy-start.2 = (bf16[2,8,8,128]{3,2,1,0:T(8,128)(2,1)}, bf16[2,8,8,128]{3,2,1,0:T(8,128)(2,1)S(1)}, u32[]{:S(2)}) copy-start(bf16[2,8,8,128]{3,2,1,0:T(8,128)(2,1)S(1)} %copy.24) | copy-start | bytes 98308
